TPU v7x, 128 devices: a whole 4x4x4 slice. The times are simulated.
128 devices in a mesh: row: 16 (over y, z), col: 8 (over x, core).
Axes of the slice: x: 4, y: 4, z: 4, core: 2. Of those that a mesh axis runs over, the one named last changes fastest.
Arguments:
- matrix_tiles: bfloat16 [16, 8, 96, 256, 256], P('row', 'col'), may hold values from -0.0546875 to 0.0546875
- tile_rows: int32 [16, 8, 96], P('row', 'col'), may hold values from 0 to 7, as said below
- tile_cols: int32 [16, 8, 96], P('row', 'col'), may hold values from 0 to 15
- tile_count: int32 [16, 8], P('row', 'col'), may hold values from 24 to 96, as said below
- x_start: float32 [32768, 256], P(('col', 'row')), may hold values from -5 to 5
- y_start: float32 [32768, 256], P(('row', 'col')), may hold values from 0 to 1
- cost_vector: float32 [32768, 256], P(('col', 'row')), may hold values from -6 to 6
- right_side: float32 [32768, 256], P(('row', 'col')), may hold values from -6 to 6
- lower_bound: float32 [32768, 256], P(('col', 'row')), may hold values from -1.5 to -0.3
- upper_bound: float32 [32768, 256], P(('col', 'row')), may hold values from 0.3 to 1.5
- step_primal: float32 [256], replicated, may hold values from 0.2 to 0.45
- step_dual: float32 [256], replicated, may hold values from 0.2 to 0.45
Outputs:
- primal_out: float32 [32768, 256], P(('col', 'row'))
- dual_out: float32 [32768, 256], P(('row', 'col'))
Inputs may be any that keep to these rules, and one draw needn't show every extreme that they name: Within one grid cell the pairs (tile_rows, tile_cols) of its slots are all different. `tile_count`: some grid cell has 96 used slots in every draw; slots at or above a cell's count are not part of A.
All inputs are finite; a program needn't handle non-finite values.
Results may differ from a plain program's by a relative error of at most 0.001.
Values may be sent and summed in bfloat16 or wider, within the bound.
No kernel may reach another device: no remote copies, remote signals or barrier semaphores. Data moves between devices by JAX's collectives and lax.ppermute only.
A program may use at most 128 MiB of HBM per device.

v0:
```python
import jax
import jax.numpy as jnp
from jax import lax
from jax.sharding import Mesh
from jax.sharding import PartitionSpec as P

NR_DEV = 8
SLOT_BLOCK = 16
ROW = ("row_0", "row_1")
COL = ("col_0", "col_1")
ROW_COL = ("row_0", "row_1", "col_0", "col_1")
COL_ROW = ("col_0", "col_1", "row_0", "row_1")
eps = 1e-06


def from_everyone(x, axis):
    devices = lax.axis_size(axis)
    return lax.all_to_all(jnp.broadcast_to(x[None], (devices, *x.shape)), axis, 0, 0, tiled=True)


def in_order(pieces, dim):
    dims = list(pieces.shape[1:])
    dims[dim] *= pieces.shape[0]
    return jnp.moveaxis(pieces, 0, dim).reshape(dims)


def gather_directly(x, axis, dim):
    pieces = from_everyone(x, axis)
    return in_order(pieces, dim)


def in_blocks(x, dim, devices):
    before, after = (x.shape[:dim], x.shape[dim + 1 :])
    return jnp.moveaxis(x.reshape(*before, devices, -1, *after), dim, 0)


def sum_at_owner(x, axis, dim):
    devices = lax.axis_size(axis)
    pieces = lax.all_to_all(in_blocks(x, dim, devices), axis, 0, 0, tiled=True)
    return jnp.sum(pieces, axis=0)


def one_axis_at_a_time(x, axes):
    for axis in axes:
        x = lax.psum(x, axis)
    return x


def forward_part(my_tiles, my_rows, my_cols, slot_count, segment):
    edge = my_tiles.shape[-1]
    batch_width = segment.shape[-1]
    x_tiles = segment.reshape(-1, edge, batch_width)
    slot_ids = jnp.arange(SLOT_BLOCK, dtype=jnp.int32)

    def forward_block_step(block_index, running):
        first_slot = block_index * SLOT_BLOCK
        tile_block = lax.dynamic_slice_in_dim(my_tiles, first_slot, SLOT_BLOCK, 0)
        row_block = lax.dynamic_slice_in_dim(my_rows, first_slot, SLOT_BLOCK, 0)
        col_block = lax.dynamic_slice_in_dim(my_cols, first_slot, SLOT_BLOCK, 0)
        in_use = first_slot + slot_ids < slot_count
        pieces = jnp.take(x_tiles, col_block, axis=0)
        products = jnp.einsum(
            "sij,sjb->sib", tile_block, pieces, preferred_element_type=jnp.float32
        )
        products = jnp.where(in_use[:, None, None], products, jnp.zeros_like(products))
        return running.at[row_block].add(products)

    blocks = (slot_count + SLOT_BLOCK - 1) // SLOT_BLOCK
    begin = jnp.zeros((NR_DEV, edge, batch_width), jnp.float32)
    return lax.fori_loop(0, blocks, forward_block_step, begin).reshape(-1, batch_width)


def backward_part(my_tiles, my_rows, my_cols, slot_count, segment, col_tiles):
    edge = my_tiles.shape[-1]
    batch_width = segment.shape[-1]
    y_tiles = segment.reshape(-1, edge, batch_width)
    slot_ids = jnp.arange(SLOT_BLOCK, dtype=jnp.int32)

    def backward_block_step(block_index, running):
        first_slot = block_index * SLOT_BLOCK
        tile_block = lax.dynamic_slice_in_dim(my_tiles, first_slot, SLOT_BLOCK, 0)
        row_block = lax.dynamic_slice_in_dim(my_rows, first_slot, SLOT_BLOCK, 0)
        col_block = lax.dynamic_slice_in_dim(my_cols, first_slot, SLOT_BLOCK, 0)
        in_use = first_slot + slot_ids < slot_count
        pieces = jnp.take(y_tiles, row_block, axis=0)
        products = jnp.einsum(
            "sij,sib->sjb", tile_block, pieces, preferred_element_type=jnp.float32
        )
        products = jnp.where(in_use[:, None, None], products, jnp.zeros_like(products))
        return running.at[col_block].add(products)

    blocks = (slot_count + SLOT_BLOCK - 1) // SLOT_BLOCK
    begin = jnp.zeros((col_tiles, edge, batch_width), jnp.float32)
    return lax.fori_loop(0, blocks, backward_block_step, begin).reshape(-1, batch_width)


def body(
    matrix_tiles,
    tile_rows,
    tile_cols,
    tile_count,
    x_start,
    y_start,
    cost_vector,
    right_side,
    lower_bound,
    upper_bound,
    step_primal,
    step_dual,
):
    my_tiles = matrix_tiles[0, 0]
    my_rows = tile_rows[0, 0]
    my_cols = tile_cols[0, 0]
    slot_count = tile_count[0, 0]
    row_devices = lax.axis_size(ROW)
    col_devices = lax.axis_size(COL)
    share = x_start.shape[0]
    edge = my_tiles.shape[-1]
    col_tiles = share * row_devices // edge
    total_cols = share * row_devices * col_devices
    total_rows = y_start.shape[0] * row_devices * col_devices

    def dual_rows(values):
        return gather_directly(values.astype(jnp.bfloat16), COL, 0)

    def row_sums(segment):
        return sum_at_owner(forward_part(my_tiles, my_rows, my_cols, slot_count, segment), COL, 0)

    x_base, cost_seg, lower_seg, upper_seg = (x_start, cost_vector, lower_bound, upper_bound)

    def column_sums(segment):
        partial_value = backward_part(my_tiles, my_rows, my_cols, slot_count, segment, col_tiles)
        return sum_at_owner(partial_value, ROW, 0)

    def spread(ahead):
        return gather_directly(ahead, ROW, 0)

    grad_zero = column_sums(dual_rows(y_start))
    primal_one = jnp.clip(x_base - step_primal * (cost_seg - grad_zero), lower_seg, upper_seg)
    primal_diff = primal_one - x_base
    move_primal = jnp.sum(primal_diff * primal_diff, axis=0)
    image_one = row_sums(spread((2.0 * primal_one - x_base).astype(jnp.bfloat16)))
    dual_one = jnp.maximum(y_start + step_dual * (right_side - image_one), 0.0)
    dual_diff = dual_one - y_start
    move_dual = jnp.sum(dual_diff * dual_diff, axis=0)
    move_primal, move_dual = (
        one_axis_at_a_time(move_primal, ROW_COL),
        one_axis_at_a_time(move_dual, ROW_COL),
    )
    weight = jnp.sqrt((move_dual / total_rows + eps) / (move_primal / total_cols + eps))
    grad_one = column_sums(dual_rows(dual_one))
    primal_two = jnp.clip(
        primal_one - step_primal / weight * (cost_seg - grad_one), lower_seg, upper_seg
    )
    image_two = row_sums(spread((2.0 * primal_two - primal_one).astype(jnp.bfloat16)))
    dual_out = jnp.maximum(dual_one + step_dual * weight * (right_side - image_two), 0.0)
    return (primal_two, dual_out)


def solution(mesh):
    torus = Mesh(mesh.devices.reshape(4, 4, 4, 2), ("row_0", "row_1", "col_0", "col_1"))
    in_specs = (
        P(ROW, COL, None, None, None),
        P(ROW, COL, None),
        P(ROW, COL, None),
        P(ROW, COL),
        P(COL_ROW, None),
        P(ROW_COL, None),
        P(COL_ROW, None),
        P(ROW_COL, None),
        P(COL_ROW, None),
        P(COL_ROW, None),
        P(),
        P(),
    )
    out_specs = (P(COL_ROW, None), P(ROW_COL, None))
    return jax.shard_map(body, mesh=torus, in_specs=in_specs, out_specs=out_specs, check_vma=False)
```

profile of v0, /device:TPU:16, one launch (start us, length us, event | category | flops | bytes accessed | tf_op | source)
XLA Modules:
  0.0 712.4 jit_solution(18077304454636752747)
XLA Ops:
  7.7 16.6 %copy.14 = bf16[96,256,256]{1,2,0:T(8,128)(2,1)} copy(bf16[96,256,256]{2,1,0:T(8,128)(2,1)} %bitcast.5) | data formatting | bytes 25165824
  26.7 92.7 %while.44 = (s32[]{:T(128)}, f32[16,256,256]{2,1,0:T(8,128)}, s32[]{:T(128)}, s32[96]{0:T(128)S(1)}, s32[]{:T(128)}, /*index=5*/bf16[96,256,256]{1,2,0:T(8,128)(...) while((s32[]{:T(128)}, f32[16,256,256]{2,1,0:T(8,128)}, ...), condition=%wide.region_2.4_spmd.clone, body=%wide.region_0.3_spmd.clone.sunk | while | flops 540017856 | bytes 25170616 | solution.py:94
  28.1 4.3 convolution_select_fusion.8
  32.5 9.5 %scatter_fusion = f32[16,256,256]{2,1,0:T(8,128)} fusion(f32[16,256,256]{2,1,0:T(8,128)} %get-tuple-element.621, s32[16]{0:T(128)S(1)} %compare_select_fusion.16, f32[16,256,256]{2,1,0:T(8,128)} %convolution_select_fusion.8), kind=kCustom, calls=%fused_computation.4.clone.clone.1 | custom fusion | flops 1048576 | bytes 12582976 | tf_op jit(solution)/shard_map/while/body/scatter-add | solution.py:90
  43.5 4.3 convolution_select_fusion.8
  47.9 9.6 %scatter_fusion = f32[16,256,256]{2,1,0:T(8,128)} fusion(f32[16,256,256]{2,1,0:T(8,128)} %get-tuple-element.621, s32[16]{0:T(128)S(1)} %compare_select_fusion.16, f32[16,256,256]{2,1,0:T(8,128)} %convolution_select_fusion.8), kind=kCustom, calls=%fused_computation.4.clone.clone.1 | custom fusion | flops 1048576 | bytes 12582976 | tf_op jit(solution)/shard_map/while/body/scatter-add | solution.py:90
  58.9 4.3 convolution_select_fusion.8
  63.3 9.7 %scatter_fusion = f32[16,256,256]{2,1,0:T(8,128)} fusion(f32[16,256,256]{2,1,0:T(8,128)} %get-tuple-element.621, s32[16]{0:T(128)S(1)} %compare_select_fusion.16, f32[16,256,256]{2,1,0:T(8,128)} %convolution_select_fusion.8), kind=kCustom, calls=%fused_computation.4.clone.clone.1 | custom fusion | flops 1048576 | bytes 12582976 | tf_op jit(solution)/shard_map/while/body/scatter-add | solution.py:90
  74.5 4.3 convolution_select_fusion.8
  78.9 9.6 %scatter_fusion = f32[16,256,256]{2,1,0:T(8,128)} fusion(f32[16,256,256]{2,1,0:T(8,128)} %get-tuple-element.621, s32[16]{0:T(128)S(1)} %compare_select_fusion.16, f32[16,256,256]{2,1,0:T(8,128)} %convolution_select_fusion.8), kind=kCustom, calls=%fused_computation.4.clone.clone.1 | custom fusion | flops 1048576 | bytes 12582976 | tf_op jit(solution)/shard_map/while/body/scatter-add | solution.py:90
  89.9 4.3 convolution_select_fusion.8
  94.4 9.8 %scatter_fusion = f32[16,256,256]{2,1,0:T(8,128)} fusion(f32[16,256,256]{2,1,0:T(8,128)} %get-tuple-element.621, s32[16]{0:T(128)S(1)} %compare_select_fusion.16, f32[16,256,256]{2,1,0:T(8,128)} %convolution_select_fusion.8), kind=kCustom, calls=%fused_computation.4.clone.clone.1 | custom fusion | flops 1048576 | bytes 12582976 | tf_op jit(solution)/shard_map/while/body/scatter-add | solution.py:90
  105.5 4.3 convolution_select_fusion.8
  110.0 9.4 %scatter_fusion = f32[16,256,256]{2,1,0:T(8,128)} fusion(f32[16,256,256]{2,1,0:T(8,128)} %get-tuple-element.621, s32[16]{0:T(128)S(1)} %compare_select_fusion.16, f32[16,256,256]{2,1,0:T(8,128)} %convolution_select_fusion.8), kind=kCustom, calls=%fused_computation.4.clone.clone.1 | custom fusion | flops 1048576 | bytes 12582976 | tf_op jit(solution)/shard_map/while/body/scatter-add | solution.py:90
  119.4 55.2 %all_to_all.40 = f32[16,256,256]{2,1,0:T(8,128)} all-to-all(f32[16,256,256]{2,1,0:T(8,128)} %get-tuple-element.196), channel_id=1, replica_groups=mesh['row_0'=4,'row_1'=4,'col_0'=4,'col_1'=2] {'row_0','row_1'}, dimensions={0} | all-to-all | bytes 8388608 | tf_op jit(solution)/shard_map/all_to_all | solution.py:39
  179.5 6.7 all-to-all-start.2
  186.2 25.3 %all-to-all-done.2 = bf16[16,256,256]{2,1,0:T(8,128)(2,1)} async-done(((bf16[16,256,256]{2,1,0:T(8,128)(2,1)}), bf16[16,256,256]{2,1,0:T(8,128)(2,1)}, u32[]{:S(2)}, u32[]{:S(2)}) %all-to-all-start.2) | async-done | bytes 2097184 | tf_op jit(solution)/shard_map/all_to_all | solution.py:18
  211.7 93.2 %while.45 = (s32[]{:T(128)}, f32[8,256,256]{2,1,0:T(8,128)S(1)}, s32[]{:T(128)}, s32[96]{0:T(128)S(1)}, s32[]{:T(128)}, /*index=5*/bf16[96,256,256]{2,1,0:T(8,12...) while((s32[]{:T(128)}, f32[8,256,256]{2,1,0:T(8,128)S(1)}, ...), condition=%wide.region_6.9_spmd.clone, body=%wide.region_4.8_spmd.clone.sunk | while | flops 540017856 | bytes 25170616 | solution.py:70
  216.0 5.0 convolution_select_fusion.9
  221.1 6.2 scatter_fusion.1
  231.6 5.0 convolution_select_fusion.9
  236.6 6.1 scatter_fusion.1
  247.1 5.0 convolution_select_fusion.9
  252.1 6.2 scatter_fusion.1
  262.6 5.0 convolution_select_fusion.9
  267.7 6.1 scatter_fusion.1
  278.1 5.0 convolution_select_fusion.9
  283.2 6.2 scatter_fusion.1
  293.7 5.0 convolution_select_fusion.9
  298.7 6.1 scatter_fusion.1
  304.9 34.1 %all_to_all.41 = f32[8,256,256]{2,1,0:T(8,128)} all-to-all(f32[8,256,256]{2,1,0:T(8,128)S(1)} %get-tuple-element.197), channel_id=1, replica_groups=mesh['row_0'=4,'row_1'=4,'col_0'=4,'col_1'=2] {'col_0','col_1'}, dimensions={0} | all-to-all | bytes 4194304 | tf_op jit(solution)/shard_map/all_to_all | solution.py:39
  345.6 15.9 %all-to-all-done.4 = bf16[8,256,256]{2,1,0:T(8,128)(2,1)S(1)} async-done(((bf16[8,256,256]{2,1,0:T(8,128)(2,1)}), bf16[8,256,256]{2,1,0:T(8,128)(2,1)S(1)}, u32[]{:S(2)}, u32[]{:S(2)}) %all-to-all-start.4) | async-done | bytes 1048608 | tf_op jit(solution)/shard_map/all_to_all | solution.py:18
  363.9 92.7 %while.46 = (s32[]{:T(128)}, f32[16,256,256]{2,1,0:T(8,128)}, s32[]{:T(128)}, s32[96]{0:T(128)S(1)}, s32[]{:T(128)}, /*index=5*/bf16[96,256,256]{1,2,0:T(8,128)(...) while((s32[]{:T(128)}, f32[16,256,256]{2,1,0:T(8,128)}, ...), condition=%wide.region_20.23_spmd.clone, body=%wide.region_18.22_spmd.clone.sunk | while | flops 540017856 | bytes 25170616 | solution.py:94
  365.3 4.3 convolution_select_fusion.10
  369.7 9.5 %scatter_fusion.2 = f32[16,256,256]{2,1,0:T(8,128)} fusion(f32[16,256,256]{2,1,0:T(8,128)} %get-tuple-element.693, s32[16]{0:T(128)S(1)} %compare_select_fusion.18, f32[16,256,256]{2,1,0:T(8,128)} %convolution_select_fusion.10), kind=kCustom, calls=%fused_computation.6.clone.clone.1 | custom fusion | flops 1048576 | bytes 12582976 | tf_op jit(solution)/shard_map/while/body/scatter-add | solution.py:90
  380.6 4.3 convolution_select_fusion.10
  385.1 9.6 %scatter_fusion.2 = f32[16,256,256]{2,1,0:T(8,128)} fusion(f32[16,256,256]{2,1,0:T(8,128)} %get-tuple-element.693, s32[16]{0:T(128)S(1)} %compare_select_fusion.18, f32[16,256,256]{2,1,0:T(8,128)} %convolution_select_fusion.10), kind=kCustom, calls=%fused_computation.6.clone.clone.1 | custom fusion | flops 1048576 | bytes 12582976 | tf_op jit(solution)/shard_map/while/body/scatter-add | solution.py:90
  396.0 4.3 convolution_select_fusion.10
  400.5 9.7 %scatter_fusion.2 = f32[16,256,256]{2,1,0:T(8,128)} fusion(f32[16,256,256]{2,1,0:T(8,128)} %get-tuple-element.693, s32[16]{0:T(128)S(1)} %compare_select_fusion.18, f32[16,256,256]{2,1,0:T(8,128)} %convolution_select_fusion.10), kind=kCustom, calls=%fused_computation.6.clone.clone.1 | custom fusion | flops 1048576 | bytes 12582976 | tf_op jit(solution)/shard_map/while/body/scatter-add | solution.py:90
  411.6 4.3 convolution_select_fusion.10
  416.0 9.6 %scatter_fusion.2 = f32[16,256,256]{2,1,0:T(8,128)} fusion(f32[16,256,256]{2,1,0:T(8,128)} %get-tuple-element.693, s32[16]{0:T(128)S(1)} %compare_select_fusion.18, f32[16,256,256]{2,1,0:T(8,128)} %convolution_select_fusion.10), kind=kCustom, calls=%fused_computation.6.clone.clone.1 | custom fusion | flops 1048576 | bytes 12582976 | tf_op jit(solution)/shard_map/while/body/scatter-add | solution.py:90
  431.5 9.8 %scatter_fusion.2 = f32[16,256,256]{2,1,0:T(8,128)} fusion(f32[16,256,256]{2,1,0:T(8,128)} %get-tuple-element.693, s32[16]{0:T(128)S(1)} %compare_select_fusion.18, f32[16,256,256]{2,1,0:T(8,128)} %convolution_select_fusion.10), kind=kCustom, calls=%fused_computation.6.clone.clone.1 | custom fusion | flops 1048576 | bytes 12582976 | tf_op jit(solution)/shard_map/while/body/scatter-add | solution.py:90
  442.7 4.3 convolution_select_fusion.10
  447.1 9.4 %scatter_fusion.2 = f32[16,256,256]{2,1,0:T(8,128)} fusion(f32[16,256,256]{2,1,0:T(8,128)} %get-tuple-element.693, s32[16]{0:T(128)S(1)} %compare_select_fusion.18, f32[16,256,256]{2,1,0:T(8,128)} %convolution_select_fusion.10), kind=kCustom, calls=%fused_computation.6.clone.clone.1 | custom fusion | flops 1048576 | bytes 12582976 | tf_op jit(solution)/shard_map/while/body/scatter-add | solution.py:90
  456.5 7.4 %all-to-all-start.5 = ((f32[16,256,256]{2,1,0:T(8,128)}), f32[16,256,256]{2,1,0:T(8,128)}, u32[]{:S(2)}, u32[]{:S(2)}) async-start(f32[16,256,256]{2,1,0:T(8,128)} %get-tuple-element.198), calls=%async_computation.5 | async-start | bytes 8388608 | tf_op jit(solution)/shard_map/all_to_all | solution.py:39
  463.9 51.3 %all-reduce.2 = (f32[256]{0:T(256)S(1)}, f32[256]{0:T(256)S(1)}) all-reduce(f32[256]{0:T(256)S(1)} %get-tuple-element.378, f32[256]{0:T(256)S(1)} %get-tuple-element.376), channel_id=1, replica_groups=mesh['row_0'=4,'row_1'=4,'col_0'=4,'col_1'=2] {'row_0'}, use_global_device_ids=true, to_apply=%region_14.17 | all-reduce | flops 512 | bytes 4096 | tf_op jit(solution)/shard_map/psum | solution.py:45
  515.3 9.3 %all-reduce.1 = (f32[256]{0:T(256)S(1)}, f32[256]{0:T(256)S(1)}) all-reduce(f32[256]{0:T(256)S(1)} %get-tuple-element.360, f32[256]{0:T(256)S(1)} %get-tuple-element.361), channel_id=1, replica_groups=mesh['row_0'=4,'row_1'=4,'col_0'=4,'col_1'=2] {'row_1'}, use_global_device_ids=true, to_apply=%region_15.18 | all-reduce | flops 512 | bytes 4096 | tf_op jit(solution)/shard_map/psum | solution.py:45
  524.6 19.5 %all-reduce = (f32[256]{0:T(256)S(1)}, f32[256]{0:T(256)S(1)}) all-reduce(f32[256]{0:T(256)S(1)} %get-tuple-element.358, f32[256]{0:T(256)S(1)} %get-tuple-element.359), channel_id=1, replica_groups=mesh['row_0'=4,'row_1'=4,'col_0'=4,'col_1'=2] {'col_0'}, use_global_device_ids=true, to_apply=%region_16.19 | all-reduce | flops 512 | bytes 4096 | tf_op jit(solution)/shard_map/psum | solution.py:45
  551.6 5.9 all-to-all-start.6
  557.5 28.2 %all-to-all-done.6 = bf16[16,256,256]{2,1,0:T(8,128)(2,1)} async-done(((bf16[16,256,256]{2,1,0:T(8,128)(2,1)}), bf16[16,256,256]{2,1,0:T(8,128)(2,1)}, u32[]{:S(2)}, u32[]{:S(2)}) %all-to-all-start.6) | async-done | bytes 2097184 | tf_op jit(solution)/shard_map/all_to_all | solution.py:18
  585.9 93.5 %while.47 = (s32[]{:T(128)}, f32[8,256,256]{2,1,0:T(8,128)S(1)}, s32[]{:T(128)}, s32[96]{0:T(128)S(1)}, s32[]{:T(128)}, /*index=5*/bf16[96,256,256]{2,1,0:T(8,12...) while((s32[]{:T(128)}, f32[8,256,256]{2,1,0:T(8,128)S(1)}, ...), condition=%wide.region_24.27_spmd.clone, body=%wide.region_22.26_spmd.clone.sunk | while | flops 540017856 | bytes 25170616 | solution.py:70
  590.5 5.0 convolution_select_fusion.11
  595.5 6.2 scatter_fusion.3
  606.0 5.0 convolution_select_fusion.11
  611.1 6.1 scatter_fusion.3
  621.6 5.0 convolution_select_fusion.11
  626.6 6.2 scatter_fusion.3
  637.2 5.0 convolution_select_fusion.11
  642.2 6.1 scatter_fusion.3
  652.7 5.0 convolution_select_fusion.11
  657.7 6.2 scatter_fusion.3
  668.3 5.0 convolution_select_fusion.11
  673.3 6.1 scatter_fusion.3
  679.5 30.4 %all_to_all.42 = f32[8,256,256]{2,1,0:T(8,128)} all-to-all(f32[8,256,256]{2,1,0:T(8,128)S(1)} %get-tuple-element.199), channel_id=1, replica_groups=mesh['row_0'=4,'row_1'=4,'col_0'=4,'col_1'=2] {'col_0','col_1'}, dimensions={0} | all-to-all | bytes 4194304 | tf_op jit(solution)/shard_map/all_to_all | solution.py:39
  (155 shorter events, 107.9 us)
Async XLA Ops:
  2.7 21.6 %all-to-all-start = ((bf16[8,256,256]{2,1,0:T(8,128)(2,1)}), bf16[8,256,256]{2,1,0:T(8,128)(2,1)S(1)}, u32[]{:S(2)}, u32[]{:S(2)}) async-start(bf16[8,256,256]{2,1,0:T(8,128)(2,1)} %broadcast_in_dim.85), calls=%async_computation | async-start | bytes 2097152 | tf_op jit(solution)/shard_map/all_to_all | solution.py:18
  24.3 2.4 copy-start.12
  24.3 2.4 copy-start.13
  174.5 2.6 copy-start.4
  174.5 2.6 copy-start.6
  174.5 2.6 copy-start.8
  174.5 2.6 copy-start.10
  174.5 2.6 copy-start.14
  177.3 0.7 copy-start
  179.5 32.0 %all-to-all-start.2 = ((bf16[16,256,256]{2,1,0:T(8,128)(2,1)}), bf16[16,256,256]{2,1,0:T(8,128)(2,1)}, u32[]{:S(2)}, u32[]{:S(2)}) async-start(bf16[16,256,256]{2,1,0:T(8,128)(2,1)} %broadcast_in_dim.86), calls=%async_computation.2 | async-start | bytes 4194304 | tf_op jit(solution)/shard_map/all_to_all | solution.py:18
  339.0 1.8 copy-start.2
  339.0 1.8 copy-start.5
  339.0 1.8 copy-start.15
  342.1 19.4 %all-to-all-start.4 = ((bf16[8,256,256]{2,1,0:T(8,128)(2,1)}), bf16[8,256,256]{2,1,0:T(8,128)(2,1)S(1)}, u32[]{:S(2)}, u32[]{:S(2)}) async-start(bf16[8,256,256]{2,1,0:T(8,128)(2,1)} %broadcast_in_dim.87), calls=%async_computation.4 | async-start | bytes 2097152 | tf_op jit(solution)/shard_map/all_to_all | solution.py:18
  456.5 90.1 %all-to-all-start.5 = ((f32[16,256,256]{2,1,0:T(8,128)}), f32[16,256,256]{2,1,0:T(8,128)}, u32[]{:S(2)}, u32[]{:S(2)}) async-start(f32[16,256,256]{2,1,0:T(8,128)} %get-tuple-element.198), calls=%async_computation.5 | async-start | bytes 8388608 | tf_op jit(solution)/shard_map/all_to_all | solution.py:39
  546.6 2.6 copy-start.1
  546.6 2.6 copy-start.7
  546.6 2.6 copy-start.9
  546.6 2.6 copy-start.11
  551.6 34.1 %all-to-all-start.6 = ((bf16[16,256,256]{2,1,0:T(8,128)(2,1)}), bf16[16,256,256]{2,1,0:T(8,128)(2,1)}, u32[]{:S(2)}, u32[]{:S(2)}) async-start(bf16[16,256,256]{2,1,0:T(8,128)(2,1)} %broadcast_in_dim.88), calls=%async_computation.6 | async-start | bytes 4194304 | tf_op jit(solution)/shard_map/all_to_all | solution.py:18
  709.8 1.8 copy-start.3
where the time goes:
time: 716 us; the launch traced here: 712 us
  other arithmetic  220 us (31%)
  blocking collectives  202 us (28%)
  matrix products  112 us (16%)
  local copies, waits for them, and re-layouts  79.1 us (11%)
  waiting for transfers between devices  69.3 us (10%)
  starting transfers between devices  27.9 us (4%)
    all_to_all x3, blocking collectives, sum_at_owner(): pieces = lax.all_to_all(in_blocks(x, dim, devices), axis, 0, 0, tiled=True)  120 us
    scatter-add x12, other arithmetic, backward_block_step(): return running.at[col_block].add(products)  115 us
    psum x4, blocking collectives, one_axis_at_a_time(): x = lax.psum(x, axis)  82.6 us
    scatter-add x12, other arithmetic, forward_block_step(): return running.at[row_block].add(products)  73.8 us
    all_to_all x4, waiting for transfers between devices, from_everyone(): lax.all_to_all(jnp.broadcast_to(x[None], (devices, *x.shape)), axis, 0, 0...  69.3 us
    dot_general x12, matrix products, forward_block_step(): jnp.einsum('sij,sjb->sib', tile_block, pieces, preferred_element_type=jnp...  59.5 us
    dot_general x12, matrix products, backward_block_step(): jnp.einsum('sij,sib->sjb', tile_block, pieces, preferred_element_type=jnp...  52.1 us
    gather x12, local copies, waits for them, and re-layouts, forward_block_step(): pieces = jnp.take(x_tiles, col_block, axis=0)  43.1 us
  transfers between devices with their start and end apart: 5, of which 3 were waited for; matrix products, arithmetic and copies ran while one was open for 2% of the time, Pallas kernels for 0%

commit v1 on v0

--- a/solution.py
+++ b/solution.py
@@ -42,7 +42,7 @@
 
 def one_axis_at_a_time(x, axes):
     for axis in axes:
-        x = lax.psum(x, axis)
+        x = jnp.sum(lax.all_gather(x, axis), axis=0)
     return x
 
 

time: 716 us -> 740 us (1.034)
  blocking collectives: 202 us -> 224 us
    all_gather x0 -> x8, blocking collectives: none -> 105 us  [one_axis_at_a_time(): x = jnp.sum(lax.all_gather(x, axis), axis=0)]
    psum x4 -> x0, blocking collectives: 82.6 us -> none  [one_axis_at_a_time(): x = lax.psum(x, axis)]
where the time goes in v1:
time: 740 us; the launch traced here: 737 us
  blocking collectives  224 us (30%)
  other arithmetic  220 us (30%)
  matrix products  112 us (15%)
  local copies, waits for them, and re-layouts  79.1 us (11%)
  waiting for transfers between devices  70.2 us (9%)
  starting transfers between devices  29.3 us (4%)
    all_to_all x3, blocking collectives, sum_at_owner(): pieces = lax.all_to_all(in_blocks(x, dim, devices), axis, 0, 0, tiled=True)  119 us
    scatter-add x12, other arithmetic, backward_block_step(): return running.at[col_block].add(products)  115 us
    all_gather x8, blocking collectives, one_axis_at_a_time(): x = jnp.sum(lax.all_gather(x, axis), axis=0)  105 us
    scatter-add x12, other arithmetic, forward_block_step(): return running.at[row_block].add(products)  73.8 us
    all_to_all x4, waiting for transfers between devices, from_everyone(): lax.all_to_all(jnp.broadcast_to(x[None], (devices, *x.shape)), axis, 0, 0...  70.2 us
    dot_general x12, matrix products, forward_block_step(): jnp.einsum('sij,sjb->sib', tile_block, pieces, preferred_element_type=jnp...  59.5 us
    dot_general x12, matrix products, backward_block_step(): jnp.einsum('sij,sib->sjb', tile_block, pieces, preferred_element_type=jnp...  52.2 us
    gather x12, local copies, waits for them, and re-layouts, forward_block_step(): pieces = jnp.take(x_tiles, col_block, axis=0)  43.1 us
  transfers between devices with their start and end apart: 5, of which 3 were waited for; matrix products, arithmetic and copies ran while one was open for 2% of the time, Pallas kernels for 0%

profile of v1, /device:TPU:16, one launch (start us, length us, event | category | flops | bytes accessed | tf_op | source)
XLA Modules:
  0.0 736.6 jit_solution(14156793891613409779)
XLA Ops:
  7.7 16.6 %copy.16 = bf16[96,256,256]{1,2,0:T(8,128)(2,1)} copy(bf16[96,256,256]{2,1,0:T(8,128)(2,1)} %bitcast.13) | data formatting | bytes 25165824
  26.7 92.6 %while.44 = (s32[]{:T(128)}, f32[16,256,256]{2,1,0:T(8,128)}, s32[]{:T(128)}, s32[96]{0:T(128)S(1)}, s32[]{:T(128)}, /*index=5*/bf16[96,256,256]{1,2,0:T(8,128)(...) while((s32[]{:T(128)}, f32[16,256,256]{2,1,0:T(8,128)}, ...), condition=%wide.region_2.4_spmd.clone, body=%wide.region_0.3_spmd.clone.sunk | while | flops 540017856 | bytes 25170616 | solution.py:94
  28.1 4.4 convolution_select_fusion.8
  32.5 9.5 %scatter_fusion = f32[16,256,256]{2,1,0:T(8,128)} fusion(f32[16,256,256]{2,1,0:T(8,128)} %get-tuple-element.629, s32[16]{0:T(128)S(1)} %compare_select_fusion.16, f32[16,256,256]{2,1,0:T(8,128)} %convolution_select_fusion.8), kind=kCustom, calls=%fused_computation.4.clone.clone.1 | custom fusion | flops 1048576 | bytes 12582976 | tf_op jit(solution)/shard_map/while/body/scatter-add | solution.py:90
  47.9 9.5 %scatter_fusion = f32[16,256,256]{2,1,0:T(8,128)} fusion(f32[16,256,256]{2,1,0:T(8,128)} %get-tuple-element.629, s32[16]{0:T(128)S(1)} %compare_select_fusion.16, f32[16,256,256]{2,1,0:T(8,128)} %convolution_select_fusion.8), kind=kCustom, calls=%fused_computation.4.clone.clone.1 | custom fusion | flops 1048576 | bytes 12582976 | tf_op jit(solution)/shard_map/while/body/scatter-add | solution.py:90
  58.8 4.4 convolution_select_fusion.8
  63.3 9.7 %scatter_fusion = f32[16,256,256]{2,1,0:T(8,128)} fusion(f32[16,256,256]{2,1,0:T(8,128)} %get-tuple-element.629, s32[16]{0:T(128)S(1)} %compare_select_fusion.16, f32[16,256,256]{2,1,0:T(8,128)} %convolution_select_fusion.8), kind=kCustom, calls=%fused_computation.4.clone.clone.1 | custom fusion | flops 1048576 | bytes 12582976 | tf_op jit(solution)/shard_map/while/body/scatter-add | solution.py:90
  74.4 4.4 convolution_select_fusion.8
  78.9 9.6 %scatter_fusion = f32[16,256,256]{2,1,0:T(8,128)} fusion(f32[16,256,256]{2,1,0:T(8,128)} %get-tuple-element.629, s32[16]{0:T(128)S(1)} %compare_select_fusion.16, f32[16,256,256]{2,1,0:T(8,128)} %convolution_select_fusion.8), kind=kCustom, calls=%fused_computation.4.clone.clone.1 | custom fusion | flops 1048576 | bytes 12582976 | tf_op jit(solution)/shard_map/while/body/scatter-add | solution.py:90
  89.9 4.4 convolution_select_fusion.8
  94.3 9.7 %scatter_fusion = f32[16,256,256]{2,1,0:T(8,128)} fusion(f32[16,256,256]{2,1,0:T(8,128)} %get-tuple-element.629, s32[16]{0:T(128)S(1)} %compare_select_fusion.16, f32[16,256,256]{2,1,0:T(8,128)} %convolution_select_fusion.8), kind=kCustom, calls=%fused_computation.4.clone.clone.1 | custom fusion | flops 1048576 | bytes 12582976 | tf_op jit(solution)/shard_map/while/body/scatter-add | solution.py:90
  105.5 4.3 convolution_select_fusion.8
  109.9 9.4 %scatter_fusion = f32[16,256,256]{2,1,0:T(8,128)} fusion(f32[16,256,256]{2,1,0:T(8,128)} %get-tuple-element.629, s32[16]{0:T(128)S(1)} %compare_select_fusion.16, f32[16,256,256]{2,1,0:T(8,128)} %convolution_select_fusion.8), kind=kCustom, calls=%fused_computation.4.clone.clone.1 | custom fusion | flops 1048576 | bytes 12582976 | tf_op jit(solution)/shard_map/while/body/scatter-add | solution.py:90
  119.3 55.2 %all_to_all.40 = f32[16,256,256]{2,1,0:T(8,128)} all-to-all(f32[16,256,256]{2,1,0:T(8,128)} %get-tuple-element.196), channel_id=1, replica_groups=mesh['row_0'=4,'row_1'=4,'col_0'=4,'col_1'=2] {'row_0','row_1'}, dimensions={0} | all-to-all | bytes 8388608 | tf_op jit(solution)/shard_map/all_to_all | solution.py:39
  179.5 6.7 all-to-all-start.2
  186.2 25.4 %all-to-all-done.2 = bf16[16,256,256]{2,1,0:T(8,128)(2,1)} async-done(((bf16[16,256,256]{2,1,0:T(8,128)(2,1)}), bf16[16,256,256]{2,1,0:T(8,128)(2,1)}, u32[]{:S(2)}, u32[]{:S(2)}) %all-to-all-start.2) | async-done | bytes 2097184 | tf_op jit(solution)/shard_map/all_to_all | solution.py:18
  211.7 93.2 %while.45 = (s32[]{:T(128)}, f32[8,256,256]{2,1,0:T(8,128)S(1)}, s32[]{:T(128)}, s32[96]{0:T(128)S(1)}, s32[]{:T(128)}, /*index=5*/bf16[96,256,256]{2,1,0:T(8,12...) while((s32[]{:T(128)}, f32[8,256,256]{2,1,0:T(8,128)S(1)}, ...), condition=%wide.region_6.9_spmd.clone, body=%wide.region_4.8_spmd.clone.sunk | while | flops 540017856 | bytes 25170616 | solution.py:70
  216.1 5.0 convolution_select_fusion.9
  221.1 6.2 scatter_fusion.1
  231.6 5.0 convolution_select_fusion.9
  236.7 6.1 scatter_fusion.1
  247.1 5.0 convolution_select_fusion.9
  252.2 6.2 scatter_fusion.1
  262.7 5.0 convolution_select_fusion.9
  267.7 6.1 scatter_fusion.1
  278.2 5.0 convolution_select_fusion.9
  283.2 6.2 scatter_fusion.1
  293.7 5.0 convolution_select_fusion.9
  298.8 6.1 scatter_fusion.1
  304.9 33.5 %all_to_all.41 = f32[8,256,256]{2,1,0:T(8,128)} all-to-all(f32[8,256,256]{2,1,0:T(8,128)S(1)} %get-tuple-element.197), channel_id=1, replica_groups=mesh['row_0'=4,'row_1'=4,'col_0'=4,'col_1'=2] {'col_0','col_1'}, dimensions={0} | all-to-all | bytes 4194304 | tf_op jit(solution)/shard_map/all_to_all | solution.py:39
  345.1 15.9 %all-to-all-done.4 = bf16[8,256,256]{2,1,0:T(8,128)(2,1)S(1)} async-done(((bf16[8,256,256]{2,1,0:T(8,128)(2,1)}), bf16[8,256,256]{2,1,0:T(8,128)(2,1)S(1)}, u32[]{:S(2)}, u32[]{:S(2)}) %all-to-all-start.4) | async-done | bytes 1048608 | tf_op jit(solution)/shard_map/all_to_all | solution.py:18
  363.3 92.6 %while.46 = (s32[]{:T(128)}, f32[16,256,256]{2,1,0:T(8,128)}, s32[]{:T(128)}, s32[96]{0:T(128)S(1)}, s32[]{:T(128)}, /*index=5*/bf16[96,256,256]{1,2,0:T(8,128)(...) while((s32[]{:T(128)}, f32[16,256,256]{2,1,0:T(8,128)}, ...), condition=%wide.region_20.23_spmd.clone, body=%wide.region_18.22_spmd.clone.sunk | while | flops 540017856 | bytes 25170616 | solution.py:94
  369.1 9.5 %scatter_fusion.2 = f32[16,256,256]{2,1,0:T(8,128)} fusion(f32[16,256,256]{2,1,0:T(8,128)} %get-tuple-element.701, s32[16]{0:T(128)S(1)} %compare_select_fusion.18, f32[16,256,256]{2,1,0:T(8,128)} %convolution_select_fusion.10), kind=kCustom, calls=%fused_computation.6.clone.clone.1 | custom fusion | flops 1048576 | bytes 12582976 | tf_op jit(solution)/shard_map/while/body/scatter-add | solution.py:90
  384.5 9.5 %scatter_fusion.2 = f32[16,256,256]{2,1,0:T(8,128)} fusion(f32[16,256,256]{2,1,0:T(8,128)} %get-tuple-element.701, s32[16]{0:T(128)S(1)} %compare_select_fusion.18, f32[16,256,256]{2,1,0:T(8,128)} %convolution_select_fusion.10), kind=kCustom, calls=%fused_computation.6.clone.clone.1 | custom fusion | flops 1048576 | bytes 12582976 | tf_op jit(solution)/shard_map/while/body/scatter-add | solution.py:90
  395.5 4.4 convolution_select_fusion.10
  399.9 9.7 %scatter_fusion.2 = f32[16,256,256]{2,1,0:T(8,128)} fusion(f32[16,256,256]{2,1,0:T(8,128)} %get-tuple-element.701, s32[16]{0:T(128)S(1)} %compare_select_fusion.18, f32[16,256,256]{2,1,0:T(8,128)} %convolution_select_fusion.10), kind=kCustom, calls=%fused_computation.6.clone.clone.1 | custom fusion | flops 1048576 | bytes 12582976 | tf_op jit(solution)/shard_map/while/body/scatter-add | solution.py:90
  411.0 4.4 convolution_select_fusion.10
  415.5 9.6 %scatter_fusion.2 = f32[16,256,256]{2,1,0:T(8,128)} fusion(f32[16,256,256]{2,1,0:T(8,128)} %get-tuple-element.701, s32[16]{0:T(128)S(1)} %compare_select_fusion.18, f32[16,256,256]{2,1,0:T(8,128)} %convolution_select_fusion.10), kind=kCustom, calls=%fused_computation.6.clone.clone.1 | custom fusion | flops 1048576 | bytes 12582976 | tf_op jit(solution)/shard_map/while/body/scatter-add | solution.py:90
  426.5 4.4 convolution_select_fusion.10
  431.0 9.7 %scatter_fusion.2 = f32[16,256,256]{2,1,0:T(8,128)} fusion(f32[16,256,256]{2,1,0:T(8,128)} %get-tuple-element.701, s32[16]{0:T(128)S(1)} %compare_select_fusion.18, f32[16,256,256]{2,1,0:T(8,128)} %convolution_select_fusion.10), kind=kCustom, calls=%fused_computation.6.clone.clone.1 | custom fusion | flops 1048576 | bytes 12582976 | tf_op jit(solution)/shard_map/while/body/scatter-add | solution.py:90
  446.5 9.4 %scatter_fusion.2 = f32[16,256,256]{2,1,0:T(8,128)} fusion(f32[16,256,256]{2,1,0:T(8,128)} %get-tuple-element.701, s32[16]{0:T(128)S(1)} %compare_select_fusion.18, f32[16,256,256]{2,1,0:T(8,128)} %convolution_select_fusion.10), kind=kCustom, calls=%fused_computation.6.clone.clone.1 | custom fusion | flops 1048576 | bytes 12582976 | tf_op jit(solution)/shard_map/while/body/scatter-add | solution.py:90
  455.9 8.0 %all-to-all-start.5 = ((f32[16,256,256]{2,1,0:T(8,128)}), f32[16,256,256]{2,1,0:T(8,128)}, u32[]{:S(2)}, u32[]{:S(2)}) async-start(f32[16,256,256]{2,1,0:T(8,128)} %get-tuple-element.198), calls=%async_computation.5 | async-start | bytes 8388608 | tf_op jit(solution)/shard_map/all_to_all | solution.py:39
  463.9 50.9 %all-gather.12 = f32[4,1,256]{2,1,0:T(1,128)S(1)} all-gather(f32[1,1,256]{2,1,0:T(1,128)S(1)} %bitcast.17), channel_id=6, replica_groups=mesh['row_0'=4,'row_1'=4,'col_0'=4,'col_1'=2] {'row_0'}, dimensions={0}, use_global_device_ids=true | all-gather | bytes 5120 | tf_op jit(solution)/shard_map/all_gather | solution.py:45
  514.8 8.3 %all-gather.13 = f32[4,1,256]{2,1,0:T(1,128)S(1)} all-gather(f32[1,1,256]{2,1,0:T(1,128)S(1)} %bitcast.18), channel_id=7, replica_groups=mesh['row_0'=4,'row_1'=4,'col_0'=4,'col_1'=2] {'row_1'}, dimensions={0}, use_global_device_ids=true | all-gather | bytes 5120 | tf_op jit(solution)/shard_map/all_gather | solution.py:45
  523.2 19.2 %all-gather.14 = f32[4,1,256]{2,1,0:T(1,128)S(1)} all-gather(f32[1,1,256]{2,1,0:T(1,128)S(1)} %bitcast.19), channel_id=8, replica_groups=mesh['row_0'=4,'row_1'=4,'col_0'=4,'col_1'=2] {'col_0'}, dimensions={0}, use_global_device_ids=true | all-gather | bytes 5120 | tf_op jit(solution)/shard_map/all_gather | solution.py:45
  544.2 8.6 %all-gather.8 = f32[4,1,256]{2,1,0:T(1,128)S(1)} all-gather(f32[1,1,256]{2,1,0:T(1,128)S(1)} %bitcast.24), channel_id=2, replica_groups=mesh['row_0'=4,'row_1'=4,'col_0'=4,'col_1'=2] {'row_0'}, dimensions={0}, use_global_device_ids=true | all-gather | bytes 5120 | tf_op jit(solution)/shard_map/all_gather | solution.py:45
  552.9 7.4 %all-gather.9 = f32[4,1,256]{2,1,0:T(1,128)S(1)} all-gather(f32[1,1,256]{2,1,0:T(1,128)S(1)} %bitcast.21), channel_id=3, replica_groups=mesh['row_0'=4,'row_1'=4,'col_0'=4,'col_1'=2] {'row_1'}, dimensions={0}, use_global_device_ids=true | all-gather | bytes 5120 | tf_op jit(solution)/shard_map/all_gather | solution.py:45
  560.3 7.0 all-gather.10
  574.2 6.9 all-to-all-start.6
  581.1 29.0 %all-to-all-done.6 = bf16[16,256,256]{2,1,0:T(8,128)(2,1)} async-done(((bf16[16,256,256]{2,1,0:T(8,128)(2,1)}), bf16[16,256,256]{2,1,0:T(8,128)(2,1)}, u32[]{:S(2)}, u32[]{:S(2)}) %all-to-all-start.6) | async-done | bytes 2097184 | tf_op jit(solution)/shard_map/all_to_all | solution.py:18
  610.2 93.5 %while.47 = (s32[]{:T(128)}, f32[8,256,256]{2,1,0:T(8,128)S(1)}, s32[]{:T(128)}, s32[96]{0:T(128)S(1)}, s32[]{:T(128)}, /*index=5*/bf16[96,256,256]{2,1,0:T(8,12...) while((s32[]{:T(128)}, f32[8,256,256]{2,1,0:T(8,128)S(1)}, ...), condition=%wide.region_24.27_spmd.clone, body=%wide.region_22.26_spmd.clone.sunk | while | flops 540017856 | bytes 25170616 | solution.py:70
  614.8 4.9 convolution_select_fusion.11
  619.8 6.2 scatter_fusion.3
  630.3 4.9 convolution_select_fusion.11
  635.4 6.1 scatter_fusion.3
  645.9 4.9 convolution_select_fusion.11
  650.9 6.2 scatter_fusion.3
  661.5 4.9 convolution_select_fusion.11
  666.5 6.1 scatter_fusion.3
  677.0 4.9 convolution_select_fusion.11
  682.0 6.2 scatter_fusion.3
  692.5 4.9 convolution_select_fusion.11
  697.6 6.1 scatter_fusion.3
  703.7 30.4 %all_to_all.42 = f32[8,256,256]{2,1,0:T(8,128)} all-to-all(f32[8,256,256]{2,1,0:T(8,128)S(1)} %get-tuple-element.199), channel_id=1, replica_groups=mesh['row_0'=4,'row_1'=4,'col_0'=4,'col_1'=2] {'col_0','col_1'}, dimensions={0} | all-to-all | bytes 4194304 | tf_op jit(solution)/shard_map/all_to_all | solution.py:39
  (167 shorter events, 122.4 us)
Async XLA Ops:
  2.7 21.6 %all-to-all-start = ((bf16[8,256,256]{2,1,0:T(8,128)(2,1)}), bf16[8,256,256]{2,1,0:T(8,128)(2,1)S(1)}, u32[]{:S(2)}, u32[]{:S(2)}) async-start(bf16[8,256,256]{2,1,0:T(8,128)(2,1)} %broadcast_in_dim.85), calls=%async_computation | async-start | bytes 2097152 | tf_op jit(solution)/shard_map/all_to_all | solution.py:18
  24.3 2.4 copy-start.12
  24.3 2.4 copy-start.13
  174.5 2.6 copy-start.4
  174.5 2.6 copy-start.6
  174.5 2.6 copy-start.8
  174.5 2.6 copy-start.10
  174.5 2.6 copy-start.14
  177.2 0.7 copy-start
  179.5 32.0 %all-to-all-start.2 = ((bf16[16,256,256]{2,1,0:T(8,128)(2,1)}), bf16[16,256,256]{2,1,0:T(8,128)(2,1)}, u32[]{:S(2)}, u32[]{:S(2)}) async-start(bf16[16,256,256]{2,1,0:T(8,128)(2,1)} %broadcast_in_dim.86), calls=%async_computation.2 | async-start | bytes 4194304 | tf_op jit(solution)/shard_map/all_to_all | solution.py:18
  338.4 1.8 copy-start.2
  338.4 1.8 copy-start.5
  338.4 1.8 copy-start.15
  341.5 19.4 %all-to-all-start.4 = ((bf16[8,256,256]{2,1,0:T(8,128)(2,1)}), bf16[8,256,256]{2,1,0:T(8,128)(2,1)S(1)}, u32[]{:S(2)}, u32[]{:S(2)}) async-start(bf16[8,256,256]{2,1,0:T(8,128)(2,1)} %broadcast_in_dim.87), calls=%async_computation.4 | async-start | bytes 2097152 | tf_op jit(solution)/shard_map/all_to_all | solution.py:18
  455.9 113.3 %all-to-all-start.5 = ((f32[16,256,256]{2,1,0:T(8,128)}), f32[16,256,256]{2,1,0:T(8,128)}, u32[]{:S(2)}, u32[]{:S(2)}) async-start(f32[16,256,256]{2,1,0:T(8,128)} %get-tuple-element.198), calls=%async_computation.5 | async-start | bytes 8388608 | tf_op jit(solution)/shard_map/all_to_all | solution.py:39
  569.2 2.6 copy-start.1
  569.2 2.6 copy-start.7
  569.2 2.6 copy-start.9
  569.2 2.6 copy-start.11
  574.2 35.9 %all-to-all-start.6 = ((bf16[16,256,256]{2,1,0:T(8,128)(2,1)}), bf16[16,256,256]{2,1,0:T(8,128)(2,1)}, u32[]{:S(2)}, u32[]{:S(2)}) async-start(bf16[16,256,256]{2,1,0:T(8,128)(2,1)} %broadcast_in_dim.88), calls=%async_computation.6 | async-start | bytes 4194304 | tf_op jit(solution)/shard_map/all_to_all | solution.py:18
  734.1 1.8 copy-start.3
